TPU v7x, 32 devices: a whole 2x2x4 slice. The times are simulated.
32 devices in a mesh: section: 2 (over core), node: 4 (over z), local: 4 (over y, x).
Axes of the slice: x: 2, y: 2, z: 4, core: 2. Of those that a mesh axis runs over, the one named last changes fastest.
Arguments:
- tokens: bfloat16 [2, 1024, 768], P(None, ('node', 'local')), may hold values from -18 to 18
- expert_ids: int32 [2, 2, 1024, 2], P('section', None, ('node', 'local')), may hold values from 0 to 15, as said below
- slots: int32 [2, 2, 1024, 2], P('section', None, ('node', 'local')), may hold values from -1 to 31, as said below
- gates: float32 [2, 2, 1024, 2], P('section', None, ('node', 'local')), may hold values from 0.2 to 1
- gain: float32 [2, 768], P('section'), may hold values from 0.5 to 1.5
- w_gate: bfloat16 [2, 16, 768, 3072], P('section', ('node', 'local')), may hold values from -0.21875 to 0.21875
- w_up: bfloat16 [2, 16, 768, 3072], P('section', ('node', 'local')), may hold values from -0.21875 to 0.21875
- w_down: bfloat16 [2, 16, 3072, 768], P('section', ('node', 'local')), may hold values from -0.109375 to 0.109375
Outputs:
- hidden: bfloat16 [2, 2, 1024, 768], P('section', None, ('node', 'local'))
Inputs may be any that keep to these rules, and one draw needn't show every extreme that they name: `expert_ids`: in each layer and micro-batch the two ids of a token differ, no expert is named by more than 256 tokens, and some expert is named by exactly 256. Expert e lies on node e // 4. Among one device's 64 tokens of a micro-batch and layer, the kept tokens that reach one node hold distinct slots below 32, and the two choices of a token on one node carry the same slot; -1 marks a dropped choice.
All inputs are finite; a program needn't handle non-finite values.
Results may differ from a plain program's by a relative error of at most 0.0085.
Values may be sent and summed in bfloat16 or wider, within the bound.
A program may use at most 64 MiB of HBM per device.

v0:
```python
import jax
import jax.numpy as jnp
from jax import lax
from jax.sharding import PartitionSpec as P


def from_behind(x, axis, by):
    count = lax.axis_size(axis)
    pairs = [(i, i + by) for i in range(count) if 0 <= i + by < count]
    return lax.ppermute(x, axis, pairs)


def rms_normed(values, gain_row):
    floats = values.astype(jnp.float32)
    mean_square = jnp.mean(floats * floats, axis=-1, keepdims=True)
    return (floats * lax.rsqrt(mean_square + 1e-05) * gain_row).astype(jnp.bfloat16)


def expert_apply(picked, matrices):
    gate_act = jnp.dot(picked, matrices[0], preferred_element_type=jnp.float32)
    up_act = jnp.dot(picked, matrices[1], preferred_element_type=jnp.float32)
    inner = (jax.nn.gelu(gate_act, approximate=True) * up_act).astype(jnp.bfloat16)
    return jnp.dot(inner, matrices[2], preferred_element_type=jnp.float32)


def weighted_terms(row_block, weight, matrices, row_limit):
    chosen = weight > 0.0
    ranked = jnp.cumsum(chosen.astype(jnp.int32)) - 1
    slot_count = min(row_limit, row_block.shape[0])
    picker = chosen[:, None] & (ranked[:, None] == jnp.arange(slot_count, dtype=jnp.int32)[None, :])
    picker_half = picker.astype(jnp.bfloat16)
    picked = jnp.dot(picker_half.T, row_block, preferred_element_type=jnp.float32).astype(
        jnp.bfloat16
    )
    picked_weight = jnp.dot(picker.astype(jnp.float32).T, weight, precision=lax.Precision.HIGHEST)
    outputs = expert_apply(picked, matrices)
    scaled = (picked_weight[:, None] * outputs).astype(jnp.bfloat16)
    return jnp.dot(picker_half, scaled, preferred_element_type=jnp.float32)


def moe_layer(layer_in, routing, slot_ids, gate_vals, gain_row, matrices):
    node_count = lax.axis_size("node")
    local_count = lax.axis_size("local")
    tok_rows = layer_in.shape[0]
    model_width = layer_in.shape[1]
    capacity = 2 * tok_rows // node_count
    row_limit = 4 * tok_rows
    normed = rms_normed(layer_in, gain_row)
    kept_mask = slot_ids >= 0
    weights_kept = jnp.where(kept_mask, gate_vals, 0.0)
    node_ids = routing // local_count
    node_slots = node_count * capacity
    slot_span = jnp.arange(node_slots, dtype=jnp.int32)
    node_pos = node_ids * capacity + slot_ids
    node_hits = [
        (node_pos[:, pick][:, None] == slot_span[None, :]) & kept_mask[:, pick][:, None]
        for pick in range(2)
    ]
    node_any = (node_hits[0] | node_hits[1]).astype(jnp.bfloat16)
    expert_count = node_count * local_count
    expert_span = jnp.arange(expert_count * capacity, dtype=jnp.int32)
    expert_pos = routing * capacity + slot_ids
    expert_hits = [
        (expert_pos[:, pick][:, None] == expert_span[None, :]) & kept_mask[:, pick][:, None]
        for pick in range(2)
    ]
    expert_any = (expert_hits[0] | expert_hits[1]).astype(jnp.bfloat16)
    packed = jnp.dot(expert_any.T, normed, preferred_element_type=jnp.float32).astype(jnp.bfloat16)
    packed = packed.reshape(expert_count, capacity, model_width)
    row_meta = jnp.sum(
        expert_hits[0].astype(jnp.float32) * weights_kept[:, 0][:, None]
        + expert_hits[1].astype(jnp.float32) * weights_kept[:, 1][:, None],
        axis=0,
    )
    row_meta = row_meta.reshape(expert_count, capacity)
    arrived = lax.all_to_all(packed, ("node", "local"), split_axis=0, concat_axis=0, tiled=True)
    arrived_meta = lax.all_to_all(
        row_meta.astype(jnp.bfloat16), ("node", "local"), split_axis=0, concat_axis=0, tiled=True
    ).astype(row_meta.dtype)
    sources = arrived.shape[0]
    item_count = arrived.shape[1]
    flat_rows = arrived.reshape(sources * item_count, model_width)
    flat_meta = arrived_meta.reshape(sources * item_count)
    term_rows = weighted_terms(flat_rows, flat_meta, matrices, row_limit)
    answer = term_rows.astype(jnp.bfloat16).reshape(sources, item_count, model_width)
    returned = lax.all_to_all(answer, ("node", "local"), split_axis=0, concat_axis=0, tiled=True)
    grouped = (
        returned.astype(jnp.float32)
        .reshape(node_count, local_count, capacity, model_width)
        .sum(axis=1)
    )
    combined_rows = grouped.astype(jnp.bfloat16).reshape(node_slots, model_width)
    mixed_rows = jnp.dot(node_any, combined_rows, preferred_element_type=jnp.float32)
    return (layer_in.astype(jnp.float32) + mixed_rows).astype(jnp.bfloat16)


def on_device(tokens, expert_ids, slots, gates, gain, w_gate, w_up, w_down):
    micro_count = tokens.shape[0]
    tok_rows = tokens.shape[1]
    model_width = tokens.shape[2]
    section_index = lax.axis_index("section")
    matrices = (w_gate[0, 0], w_up[0, 0], w_down[0, 0])
    gain_row = gain[0]
    results = jnp.zeros((micro_count, tok_rows, model_width), jnp.bfloat16)
    carried = jnp.zeros((tok_rows, model_width), jnp.bfloat16)
    for step_index in range(micro_count + 1):
        fresh_rows = tokens[min(step_index, micro_count - 1)]
        layer_in = jnp.where(section_index == 0, fresh_rows, carried)
        offset = step_index - section_index
        batch_index = jnp.clip(offset, 0, micro_count - 1)
        routing = lax.dynamic_index_in_dim(expert_ids[0], batch_index, 0, keepdims=False)
        slot_ids = lax.dynamic_index_in_dim(slots[0], batch_index, 0, keepdims=False)
        gate_vals = lax.dynamic_index_in_dim(gates[0], batch_index, 0, keepdims=False)
        layer_out = moe_layer(layer_in, routing, slot_ids, gate_vals, gain_row, matrices)
        valid_tick = (offset >= 0) & (offset < micro_count)
        updated = lax.dynamic_update_index_in_dim(results, layer_out, batch_index, 0)
        results = jnp.where(valid_tick, updated, results)
        if step_index < micro_count:
            carried = from_behind(layer_out, "section", 1)
    return results[None]


def solution(mesh):
    placed = (
        P(None, ("node", "local"), None),
        P("section", None, ("node", "local"), None),
        P("section", None, ("node", "local"), None),
        P("section", None, ("node", "local"), None),
        P("section", None),
        P("section", ("node", "local"), None, None),
        P("section", ("node", "local"), None, None),
        P("section", ("node", "local"), None, None),
    )
    return jax.shard_map(
        on_device,
        mesh=mesh,
        in_specs=placed,
        out_specs=P("section", None, ("node", "local"), None),
        check_vma=False,
    )
```

profile of v0, /device:TPU:0, one launch (start us, length us, event | category | flops | bytes accessed | tf_op | source)
XLA Modules:
  0.0 221.2 jit_solution(4656817201888473145)
XLA Ops:
  2.4 8.3 %all-to-all-start = ((bf16[16,1,32]{2,1,0:T(2,128)(2,1)}), bf16[16,1,32]{2,1,0:T(2,128)(2,1)S(1)}, u32[]{:S(2)}, u32[]{:S(2)}) async-start(bf16[16,1,32]{2,1,0:T(2,128)(2,1)} %convert_element_type.269), calls=%async_computation | async-start | bytes 16384 | tf_op jit(solution)/shard_map/all_to_all | solution.py:77
  13.4 4.6 %all-to-all-done = bf16[16,1,32]{2,1,0:T(2,128)(2,1)S(1)} async-done(((bf16[16,1,32]{2,1,0:T(2,128)(2,1)}), bf16[16,1,32]{2,1,0:T(2,128)(2,1)S(1)}, u32[]{:S(2)}, u32[]{:S(2)}) %all-to-all-start) | async-done | bytes 1056 | tf_op jit(solution)/shard_map/all_to_all | solution.py:77
  18.0 3.5 %all-to-all-start.3 = ((bf16[16,1,32]{2,1,0:T(2,128)(2,1)}), bf16[16,1,32]{2,1,0:T(2,128)(2,1)S(1)}, u32[]{:S(2)}, u32[]{:S(2)}) async-start(bf16[16,1,32]{2,1,0:T(2,128)(2,1)} %convert_element_type.270), calls=%async_computation.3 | async-start | bytes 16384 | tf_op jit(solution)/shard_map/all_to_all | solution.py:77
  21.5 2.3 %convolution_convert_fusion.5 = bf16[512,768]{1,0:T(8,128)(2,1)} fusion(f32[768]{0:T(1024)S(1)} %reduce.7, f32[64]{0:T(128)S(1)} %add_rsqrt_fusion.2, s32[64]{0:T(128)S(1)} %get-tuple-element.42, s32[64]{0:T(128)S(1)} %get-tuple-element.41, pred[64]{0:T(512)(128)(4,1)S(1)} %get-tuple-element.48, pred[64]{0:T(512)(128)(4,1)S(1)} %get-tuple-element.47, ...), kind=kOutput, calls=%fused_computation.53 | convolution fusion | flops 51134464 | bytes 888705 | tf_op jit(solution)/shard_map/dot_general | solution.py:68
  23.8 5.0 %all-to-all-done.3 = bf16[16,1,32]{2,1,0:T(2,128)(2,1)S(1)} async-done(((bf16[16,1,32]{2,1,0:T(2,128)(2,1)}), bf16[16,1,32]{2,1,0:T(2,128)(2,1)S(1)}, u32[]{:S(2)}, u32[]{:S(2)}) %all-to-all-start.3) | async-done | bytes 1056 | tf_op jit(solution)/shard_map/all_to_all | solution.py:77
  28.7 3.6 %all-to-all-start.1 = ((bf16[16,32,768]{2,1,0:T(8,128)(2,1)}), bf16[16,32,768]{2,1,0:T(8,128)(2,1)S(1)}, u32[]{:S(2)}, u32[]{:S(2)}) async-start(bf16[16,32,768]{2,1,0:T(8,128)(2,1)} %bitcast.15), calls=%async_computation.1 | async-start | bytes 1572864 | tf_op jit(solution)/shard_map/all_to_all | solution.py:76
  33.6 16.7 %all-to-all-done.1 = bf16[16,32,768]{2,1,0:T(8,128)(2,1)S(1)} async-done(((bf16[16,32,768]{2,1,0:T(8,128)(2,1)}), bf16[16,32,768]{2,1,0:T(8,128)(2,1)S(1)}, u32[]{:S(2)}, u32[]{:S(2)}) %all-to-all-start.1) | async-done | bytes 786464 | tf_op jit(solution)/shard_map/all_to_all | solution.py:76
  50.9 4.6 %fusion.42 = f32[256,3072]{1,0:T(8,128)S(1)} fusion(bf16[256,768]{1,0:T(8,128)(2,1)S(1)} %convolution_convert_fusion.8, bf16[1,1,768,3072]{3,2,1,0:T(8,128)(2,1)} %param.13), kind=kOutput, calls=%fused_computation.33 | convolution fusion | flops 1214251008 | bytes 8257536 | tf_op jit(solution)/shard_map/dot_general | solution.py:20
  55.6 1.4 fusion.33
  57.0 5.1 %convolution_convert_fusion.4 = bf16[512,768]{1,0:T(8,128)(2,1)} fusion(bf16[256,3072]{1,0:T(8,128)(2,1)S(1)} %fusion.33, bf16[1,1,3072,768]{3,2,1,0:T(8,128)(2,1)} %param.15, f32[256]{0:T(256)S(1)} %bitcast.252, s32[512]{0:T(512)S(1)} %add_bitcast_fusion.2, pred[512]{0:T(512)(128)(4,1)S(1)} %convert_compare_fusion.2), kind=kOutput, calls=%fused_computation.52 | convolution fusion | flops 1410334720 | bytes 7081472 | tf_op jit(solution)/shard_map/dot_general | solution.py:38
  62.1 4.3 %all-to-all-start.2 = ((bf16[16,32,768]{2,1,0:T(8,128)(2,1)}), bf16[16,32,768]{2,1,0:T(8,128)(2,1)S(1)}, u32[]{:S(2)}, u32[]{:S(2)}) async-start(bf16[16,32,768]{2,1,0:T(8,128)(2,1)} %bitcast.20), calls=%async_computation.2 | async-start | bytes 1572864 | tf_op jit(solution)/shard_map/all_to_all | solution.py:86
  66.4 18.5 %all-to-all-done.2 = bf16[16,32,768]{2,1,0:T(8,128)(2,1)S(1)} async-done(((bf16[16,32,768]{2,1,0:T(8,128)(2,1)}), bf16[16,32,768]{2,1,0:T(8,128)(2,1)S(1)}, u32[]{:S(2)}, u32[]{:S(2)}) %all-to-all-start.2) | async-done | bytes 786464 | tf_op jit(solution)/shard_map/all_to_all | solution.py:86
  85.3 1.3 collective-permute-start
  87.6 1.4 convolution_convert_fusion.3
  89.0 4.6 %all-to-all-start.4 = ((bf16[16,32,768]{2,1,0:T(8,128)(2,1)}), bf16[16,32,768]{2,1,0:T(8,128)(2,1)S(1)}, u32[]{:S(2)}, u32[]{:S(2)}) async-start(bf16[16,32,768]{2,1,0:T(8,128)(2,1)} %bitcast.38), calls=%async_computation.4 | async-start | bytes 1572864 | tf_op jit(solution)/shard_map/all_to_all | solution.py:76
  94.7 19.0 %all-to-all-done.4 = bf16[16,32,768]{2,1,0:T(8,128)(2,1)S(1)} async-done(((bf16[16,32,768]{2,1,0:T(8,128)(2,1)}), bf16[16,32,768]{2,1,0:T(8,128)(2,1)S(1)}, u32[]{:S(2)}, u32[]{:S(2)}) %all-to-all-start.4) | async-done | bytes 786464 | tf_op jit(solution)/shard_map/all_to_all | solution.py:76
  114.3 4.6 %fusion.51 = f32[256,3072]{1,0:T(8,128)S(1)} fusion(bf16[256,768]{1,0:T(8,128)(2,1)S(1)} %convolution_convert_fusion.7, bf16[1,1,768,3072]{3,2,1,0:T(8,128)(2,1)} %param.13), kind=kOutput, calls=%fused_computation.40 | convolution fusion | flops 1214251008 | bytes 8257536 | tf_op jit(solution)/shard_map/dot_general | solution.py:20
  119.0 1.4 fusion.30
  120.4 5.1 %convolution_convert_fusion.2 = bf16[512,768]{1,0:T(8,128)(2,1)} fusion(bf16[256,3072]{1,0:T(8,128)(2,1)S(1)} %fusion.30, bf16[1,1,3072,768]{3,2,1,0:T(8,128)(2,1)} %param.15, f32[256]{0:T(256)S(1)} %bitcast.253, s32[512]{0:T(512)S(1)} %add_bitcast_fusion.1, pred[512]{0:T(512)(128)(4,1)S(1)} %convert_compare_fusion.1), kind=kOutput, calls=%fused_computation.50 | convolution fusion | flops 1410334720 | bytes 7081472 | tf_op jit(solution)/shard_map/dot_general | solution.py:38
  125.4 5.1 %all-to-all-start.5 = ((bf16[16,32,768]{2,1,0:T(8,128)(2,1)}), bf16[16,32,768]{2,1,0:T(8,128)(2,1)S(1)}, u32[]{:S(2)}, u32[]{:S(2)}) async-start(bf16[16,32,768]{2,1,0:T(8,128)(2,1)} %bitcast.40), calls=%async_computation.5 | async-start | bytes 1572864 | tf_op jit(solution)/shard_map/all_to_all | solution.py:86
  130.6 18.7 %all-to-all-done.5 = bf16[16,32,768]{2,1,0:T(8,128)(2,1)S(1)} async-done(((bf16[16,32,768]{2,1,0:T(8,128)(2,1)}), bf16[16,32,768]{2,1,0:T(8,128)(2,1)S(1)}, u32[]{:S(2)}, u32[]{:S(2)}) %all-to-all-start.5) | async-done | bytes 786464 | tf_op jit(solution)/shard_map/all_to_all | solution.py:86
  149.7 1.3 collective-permute-start.1
  151.8 5.0 %all-to-all-start.6 = ((bf16[16,1,32]{2,1,0:T(2,128)(2,1)}), bf16[16,1,32]{2,1,0:T(2,128)(2,1)S(1)}, u32[]{:S(2)}, u32[]{:S(2)}) async-start(bf16[16,1,32]{2,1,0:T(2,128)(2,1)} %convert_element_type.271), calls=%async_computation.6 | async-start | bytes 16384 | tf_op jit(solution)/shard_map/all_to_all | solution.py:77
  156.9 1.4 convolution_convert_fusion.1
  158.3 5.7 %all-to-all-done.6 = bf16[16,1,32]{2,1,0:T(2,128)(2,1)S(1)} async-done(((bf16[16,1,32]{2,1,0:T(2,128)(2,1)}), bf16[16,1,32]{2,1,0:T(2,128)(2,1)S(1)}, u32[]{:S(2)}, u32[]{:S(2)}) %all-to-all-start.6) | async-done | bytes 1056 | tf_op jit(solution)/shard_map/all_to_all | solution.py:77
  164.0 3.6 %all-to-all-start.7 = ((bf16[16,32,768]{2,1,0:T(8,128)(2,1)}), bf16[16,32,768]{2,1,0:T(8,128)(2,1)S(1)}, u32[]{:S(2)}, u32[]{:S(2)}) async-start(bf16[16,32,768]{2,1,0:T(8,128)(2,1)} %bitcast.58), calls=%async_computation.7 | async-start | bytes 1572864 | tf_op jit(solution)/shard_map/all_to_all | solution.py:76
  168.8 16.8 %all-to-all-done.7 = bf16[16,32,768]{2,1,0:T(8,128)(2,1)S(1)} async-done(((bf16[16,32,768]{2,1,0:T(8,128)(2,1)}), bf16[16,32,768]{2,1,0:T(8,128)(2,1)S(1)}, u32[]{:S(2)}, u32[]{:S(2)}) %all-to-all-start.7) | async-done | bytes 786464 | tf_op jit(solution)/shard_map/all_to_all | solution.py:76
  186.2 4.6 %fusion.60 = f32[256,3072]{1,0:T(8,128)S(1)} fusion(bf16[256,768]{1,0:T(8,128)(2,1)S(1)} %convolution_convert_fusion.6, bf16[1,1,768,3072]{3,2,1,0:T(8,128)(2,1)} %param.13), kind=kOutput, calls=%fused_computation.47 | convolution fusion | flops 1214251008 | bytes 8257536 | tf_op jit(solution)/shard_map/dot_general | solution.py:20
  190.9 1.4 fusion.27
  192.3 5.1 %convolution_convert_fusion = bf16[512,768]{1,0:T(8,128)(2,1)} fusion(bf16[256,3072]{1,0:T(8,128)(2,1)S(1)} %fusion.27, bf16[1,1,3072,768]{3,2,1,0:T(8,128)(2,1)} %param.15, f32[256]{0:T(256)S(1)} %bitcast.254, s32[512]{0:T(512)S(1)} %add_bitcast_fusion, pred[512]{0:T(512)(128)(4,1)S(1)} %convert_compare_fusion), kind=kOutput, calls=%fused_computation.48 | convolution fusion | flops 1410334720 | bytes 7081472 | tf_op jit(solution)/shard_map/dot_general | solution.py:38
  197.3 4.3 %all-to-all-start.8 = ((bf16[16,32,768]{2,1,0:T(8,128)(2,1)}), bf16[16,32,768]{2,1,0:T(8,128)(2,1)S(1)}, u32[]{:S(2)}, u32[]{:S(2)}) async-start(bf16[16,32,768]{2,1,0:T(8,128)(2,1)} %bitcast.60), calls=%async_computation.8 | async-start | bytes 1572864 | tf_op jit(solution)/shard_map/all_to_all | solution.py:86
  202.4 17.8 %all-to-all-done.8 = bf16[16,32,768]{2,1,0:T(8,128)(2,1)S(1)} async-done(((bf16[16,32,768]{2,1,0:T(8,128)(2,1)}), bf16[16,32,768]{2,1,0:T(8,128)(2,1)S(1)}, u32[]{:S(2)}, u32[]{:S(2)}) %all-to-all-start.8) | async-done | bytes 786464 | tf_op jit(solution)/shard_map/all_to_all | solution.py:86
  (92 shorter events, 14.6 us)
Async XLA Ops:
  2.4 15.6 %all-to-all-start = ((bf16[16,1,32]{2,1,0:T(2,128)(2,1)}), bf16[16,1,32]{2,1,0:T(2,128)(2,1)S(1)}, u32[]{:S(2)}, u32[]{:S(2)}) async-start(bf16[16,1,32]{2,1,0:T(2,128)(2,1)} %convert_element_type.269), calls=%async_computation | async-start | bytes 16384 | tf_op jit(solution)/shard_map/all_to_all | solution.py:77
  18.0 10.7 %all-to-all-start.3 = ((bf16[16,1,32]{2,1,0:T(2,128)(2,1)}), bf16[16,1,32]{2,1,0:T(2,128)(2,1)S(1)}, u32[]{:S(2)}, u32[]{:S(2)}) async-start(bf16[16,1,32]{2,1,0:T(2,128)(2,1)} %convert_element_type.270), calls=%async_computation.3 | async-start | bytes 16384 | tf_op jit(solution)/shard_map/all_to_all | solution.py:77
  28.7 21.5 %all-to-all-start.1 = ((bf16[16,32,768]{2,1,0:T(8,128)(2,1)}), bf16[16,32,768]{2,1,0:T(8,128)(2,1)S(1)}, u32[]{:S(2)}, u32[]{:S(2)}) async-start(bf16[16,32,768]{2,1,0:T(8,128)(2,1)} %bitcast.15), calls=%async_computation.1 | async-start | bytes 1572864 | tf_op jit(solution)/shard_map/all_to_all | solution.py:76
  50.3 5.2 %slice-start = ((s8[4718592]{0:T(1024)(128)(4,1)}), s8[4194304]{0:T(1024)(128)(4,1)S(1)}, s32[]{:S(2)}) async-start(s8[4718592]{0:T(1024)(128)(4,1)} %bitcast.239), calls=%async_computation.9 | async-start | bytes 8388608
  50.9 4.7 %slice-start.1 = ((s8[4718592]{0:T(1024)(128)(4,1)}), s8[524288]{0:T(1024)(128)(4,1)S(1)}, s32[]{:S(2)}) async-start(s8[4718592]{0:T(1024)(128)(4,1)} %bitcast.239), calls=%async_computation.10 | async-start | bytes 1048576
  57.0 28.1 %copy-start = (bf16[2,64,768]{2,1,0:T(8,128)(2,1)S(1)}, bf16[2,64,768]{2,1,0:T(8,128)(2,1)}, u32[]{:S(2)}) copy-start(bf16[2,64,768]{2,1,0:T(8,128)(2,1)} %param.8) | copy-start | bytes 589828
  62.1 22.8 %all-to-all-start.2 = ((bf16[16,32,768]{2,1,0:T(8,128)(2,1)}), bf16[16,32,768]{2,1,0:T(8,128)(2,1)S(1)}, u32[]{:S(2)}, u32[]{:S(2)}) async-start(bf16[16,32,768]{2,1,0:T(8,128)(2,1)} %bitcast.20), calls=%async_computation.2 | async-start | bytes 1572864 | tf_op jit(solution)/shard_map/all_to_all | solution.py:86
  85.3 2.2 %collective-permute-start = (bf16[64,768]{1,0:T(8,128)(2,1)S(1)}, bf16[64,768]{1,0:T(8,128)(2,1)S(1)}, u32[]{:S(2)}, u32[]{:S(2)}) collective-permute-start(bf16[64,768]{1,0:T(8,128)(2,1)S(1)} %get-tuple-element.50), channel_id=1, source_target_pairs={{0,16},{1,17},{2,18},{3,19},{4,20},{5,21},{6,22},{7,23},{8,24},{9,... | collective-permute-start | bytes 294920 | tf_op jit(solution)/shard_map/ppermute | solution.py:10
  89.0 24.7 %all-to-all-start.4 = ((bf16[16,32,768]{2,1,0:T(8,128)(2,1)}), bf16[16,32,768]{2,1,0:T(8,128)(2,1)S(1)}, u32[]{:S(2)}, u32[]{:S(2)}) async-start(bf16[16,32,768]{2,1,0:T(8,128)(2,1)} %bitcast.38), calls=%async_computation.4 | async-start | bytes 1572864 | tf_op jit(solution)/shard_map/all_to_all | solution.py:76
  113.7 5.2 %slice-start.2 = ((s8[4718592]{0:T(1024)(128)(4,1)}), s8[4194304]{0:T(1024)(128)(4,1)S(1)}, s32[]{:S(2)}) async-start(s8[4718592]{0:T(1024)(128)(4,1)} %bitcast.241), calls=%async_computation.11 | async-start | bytes 8388608
  114.3 4.7 %slice-start.3 = ((s8[4718592]{0:T(1024)(128)(4,1)}), s8[524288]{0:T(1024)(128)(4,1)S(1)}, s32[]{:S(2)}) async-start(s8[4718592]{0:T(1024)(128)(4,1)} %bitcast.241), calls=%async_computation.12 | async-start | bytes 1048576
  125.4 23.9 %all-to-all-start.5 = ((bf16[16,32,768]{2,1,0:T(8,128)(2,1)}), bf16[16,32,768]{2,1,0:T(8,128)(2,1)S(1)}, u32[]{:S(2)}, u32[]{:S(2)}) async-start(bf16[16,32,768]{2,1,0:T(8,128)(2,1)} %bitcast.40), calls=%async_computation.5 | async-start | bytes 1572864 | tf_op jit(solution)/shard_map/all_to_all | solution.py:86
  149.7 7.1 %collective-permute-start.1 = (bf16[64,768]{1,0:T(8,128)(2,1)S(1)}, bf16[64,768]{1,0:T(8,128)(2,1)S(1)}, u32[]{:S(2)}, u32[]{:S(2)}) collective-permute-start(bf16[64,768]{1,0:T(8,128)(2,1)S(1)} %get-tuple-element.52), channel_id=1, source_target_pairs={{0,16},{1,17},{2,18},{3,19},{4,20},{5,21},{6,22},{7,23},{8,24},{9,... | collective-permute-start | bytes 294920 | tf_op jit(solution)/shard_map/ppermute | solution.py:10
  151.8 12.2 %all-to-all-start.6 = ((bf16[16,1,32]{2,1,0:T(2,128)(2,1)}), bf16[16,1,32]{2,1,0:T(2,128)(2,1)S(1)}, u32[]{:S(2)}, u32[]{:S(2)}) async-start(bf16[16,1,32]{2,1,0:T(2,128)(2,1)} %convert_element_type.271), calls=%async_computation.6 | async-start | bytes 16384 | tf_op jit(solution)/shard_map/all_to_all | solution.py:77
  164.0 21.6 %all-to-all-start.7 = ((bf16[16,32,768]{2,1,0:T(8,128)(2,1)}), bf16[16,32,768]{2,1,0:T(8,128)(2,1)S(1)}, u32[]{:S(2)}, u32[]{:S(2)}) async-start(bf16[16,32,768]{2,1,0:T(8,128)(2,1)} %bitcast.58), calls=%async_computation.7 | async-start | bytes 1572864 | tf_op jit(solution)/shard_map/all_to_all | solution.py:76
  185.6 5.2 %slice-start.4 = ((s8[4718592]{0:T(1024)(128)(4,1)}), s8[4194304]{0:T(1024)(128)(4,1)S(1)}, s32[]{:S(2)}) async-start(s8[4718592]{0:T(1024)(128)(4,1)} %bitcast.243), calls=%async_computation.13 | async-start | bytes 8388608
  186.2 4.7 %slice-start.5 = ((s8[4718592]{0:T(1024)(128)(4,1)}), s8[524288]{0:T(1024)(128)(4,1)S(1)}, s32[]{:S(2)}) async-start(s8[4718592]{0:T(1024)(128)(4,1)} %bitcast.243), calls=%async_computation.14 | async-start | bytes 1048576
  197.3 22.8 %all-to-all-start.8 = ((bf16[16,32,768]{2,1,0:T(8,128)(2,1)}), bf16[16,32,768]{2,1,0:T(8,128)(2,1)S(1)}, u32[]{:S(2)}, u32[]{:S(2)}) async-start(bf16[16,32,768]{2,1,0:T(8,128)(2,1)} %bitcast.60), calls=%async_computation.8 | async-start | bytes 1572864 | tf_op jit(solution)/shard_map/all_to_all | solution.py:86
where the time goes:
time: 222 us; the launch traced here: 221 us
  waiting for transfers between devices  124 us (56%)
  starting transfers between devices  44.9 us (20%)
  matrix products  42.1 us (19%)
  other arithmetic  5.76 us (3%)
  local copies, waits for them, and re-layouts  4.19 us (2%)
    all_to_all x3, waiting for transfers between devices, moe_layer(): lax.all_to_all(answer, ('node', 'local'), split_axis=0, concat_axis=0, ti...  55 us
    all_to_all x3, waiting for transfers between devices, moe_layer(): lax.all_to_all(packed, ('node', 'local'), split_axis=0, concat_axis=0, ti...  52.5 us
    all_to_all x3, starting transfers between devices, moe_layer(): lax.all_to_all(row_meta.astype(jnp.bfloat16), ('node', 'local'), split_ax...  16.8 us
    all_to_all x3, waiting for transfers between devices, moe_layer(): lax.all_to_all(row_meta.astype(jnp.bfloat16), ('node', 'local'), split_ax...  15.3 us
    dot_general x3, matrix products, weighted_terms(): return jnp.dot(picker_half, scaled, preferred_element_type=jnp.float32)  15.3 us
    dot_general x3, matrix products, expert_apply(): gate_act = jnp.dot(picked, matrices[0], preferred_element_type=jnp.float32)  13.9 us
    all_to_all x3, starting transfers between devices, moe_layer(): lax.all_to_all(answer, ('node', 'local'), split_axis=0, concat_axis=0, ti...  13.8 us
    all_to_all x3, starting transfers between devices, moe_layer(): lax.all_to_all(packed, ('node', 'local'), split_axis=0, concat_axis=0, ti...  11.8 us
  transfers between devices with their start and end apart: 11, of which 10 were waited for; matrix products, arithmetic and copies ran while one was open for 5% of the time, Pallas kernels for 0%

commit v1 on v0

v1 whole, which is shorter than its diff:
```python
import functools

import jax
import jax.numpy as jnp
from jax import lax
from jax.experimental import pallas as pl
from jax.experimental.pallas import tpu as pltpu
from jax.sharding import PartitionSpec as P

MESH = pl.DeviceIdType.MESH
LANES = 128
FF_CHUNKS = 3


def over_rows(a, b, precision=None):
    return lax.dot_general(
        a, b, (((0,), (0,)), ((), ())), precision=precision, preferred_element_type=jnp.float32
    )


def relay_kernel(
    sizes,
    tok_ref, ids_ref, slots_ref, gates_ref, gain_ref, wg_hbm, wu_hbm, wd_hbm,
    out_ref,
    held, packed, arrived, answer, returned, hits, meta_out, meta_in, pick, pick_w, acc,
    wg, wu, wd,
    w_sem, meta_send, meta_recv, d_send, d_recv, r_send, r_recv, relay_send, relay_recv,
):
    n_sec, n_node, n_local, micro, toks, width, cap, limit = sizes
    n = n_node * n_local
    total = n * cap
    groups = total // LANES
    sec = lax.axis_index("section")
    node = lax.axis_index("node")
    local = lax.axis_index("local")
    me = node * n_local + local

    def device(p):
        return {"node": lax.div(p, n_local), "local": lax.rem(p, n_local)}

    def peers(body):
        lax.fori_loop(1, n, lambda i, c: (body(lax.rem(me + i, n)), c)[1], 0)

    barrier = pltpu.get_barrier_semaphore()
    peers(lambda p: pl.semaphore_signal(barrier, inc=1, device_id=device(p), device_id_type=MESH))
    for i in range(1, n_sec):
        pl.semaphore_signal(
            barrier, inc=1, device_id={"section": lax.rem(sec + i, n_sec)}, device_id_type=MESH
        )

    def weight_copies(c):
        chunk = wg.shape[2]
        cols = pl.ds(pl.multiple_of(c * chunk, chunk), chunk)
        return (
            pltpu.make_async_copy(wg_hbm.at[:, cols], wg.at[c], w_sem.at[0, c]),
            pltpu.make_async_copy(wu_hbm.at[:, cols], wu.at[c], w_sem.at[1, c]),
            pltpu.make_async_copy(wd_hbm.at[cols, :], wd.at[c], w_sem.at[2, c]),
        )

    for c in range(FF_CHUNKS):
        for copy in weight_copies(c):
            copy.start()

    def meta_copy(p):
        return pltpu.make_async_remote_copy(
            meta_out.at[p], meta_in.at[me], meta_send.at[p], meta_recv.at[me],
            device_id=device(p), device_id_type=MESH,
        )

    def out_copy(mb, p):
        return pltpu.make_async_remote_copy(
            packed.at[mb, lax.div(p, n_local)], arrived.at[mb, me], d_send.at[mb, p],
            d_recv.at[mb, me], device_id=device(p), device_id_type=MESH,
        )

    def back_copy(mb, p):
        return pltpu.make_async_remote_copy(
            answer.at[mb, p], returned.at[mb, me], r_send.at[mb, p],
            r_recv.at[mb, me], device_id=device(p), device_id_type=MESH,
        )

    def arrival(buffer, sem, p):
        return pltpu.make_async_remote_copy(
            buffer.at[p], buffer.at[p], sem.at[p], sem.at[p],
            device_id=device(p), device_id_type=MESH,
        )

    def relay_copy(mb):
        return pltpu.make_async_remote_copy(
            out_ref.at[mb], held.at[mb], relay_send.at[mb], relay_recv.at[mb],
            device_id={"section": lax.rem(sec + 1, n_sec)}, device_id_type=MESH,
        )

    slot_span = lax.broadcasted_iota(jnp.int32, (toks, n_node * cap), 1)
    exp_span = lax.broadcasted_iota(jnp.int32, (toks, n), 1)
    lane_span = lax.broadcasted_iota(jnp.int32, (toks, LANES), 1)
    row_span = lax.broadcasted_iota(jnp.int32, (n, micro * groups, LANES), 1)
    my_group = lax.div(me * cap, LANES)
    my_lane = lax.rem(me * cap, LANES)
    meta = jnp.zeros((n, micro * groups, LANES), jnp.float32)
    for mb in range(micro):
        hit = None
        weights = None
        for k in range(2):
            e = ids_ref[mb, :, k : k + 1]
            s = slots_ref[mb, :, k : k + 1]
            g = gates_ref[mb, :, k : k + 1]
            pos = jnp.where(s >= 0, lax.div(e, jnp.full_like(e, n_local)) * cap + s, -1)
            this = jnp.where(pos == slot_span, 1.0, 0.0)
            hit = this if hit is None else jnp.maximum(hit, this)
            lane = jnp.where(s >= 0, my_lane + s, -1)
            part = over_rows(
                jnp.where(e == exp_span, g, 0.0),
                jnp.where(lane == lane_span, 1.0, 0.0),
                lax.Precision.HIGHEST,
            )
            weights = part if weights is None else weights + part
        hits[mb] = hit.astype(jnp.bfloat16)
        meta = meta + jnp.where(row_span == mb * groups + my_group, weights[:, None, :], 0.0)
    meta_out[...] = meta
    meta_in[me] = meta_out[me]

    def pack(mb, h):
        floats = h.astype(jnp.float32)
        mean_square = jnp.mean(floats * floats, axis=-1, keepdims=True)
        normed = (floats * lax.rsqrt(mean_square + 1e-05) * gain_ref[...]).astype(jnp.bfloat16)
        rows = over_rows(hits[mb], normed)
        for j in range(n_node):
            packed[mb, j] = rows[j * cap : (j + 1) * cap].astype(jnp.bfloat16)
        arrived[mb, me] = packed[mb, node]

    @pl.when(sec == 0)
    def _():
        held[...] = tok_ref[...]
        pack(0, held[0])

    pl.semaphore_wait(barrier, n - 1 + n_sec - 1)
    peers(lambda p: meta_copy(p).start())

    @pl.when(sec == 0)
    def _():
        peers(lambda p: out_copy(0, p).start())
        for mb in range(1, micro):
            pack(mb, held[mb])
            peers(lambda p: out_copy(mb, p).start())

    peers(lambda p: arrival(meta_in, meta_recv, p).wait_recv())
    meta = jnp.sum(meta_in[...], axis=0)
    upto = lax.broadcasted_iota(jnp.int32, (total, total), 0) <= lax.broadcasted_iota(
        jnp.int32, (total, total), 1
    )
    upto = jnp.where(upto, 1.0, 0.0).astype(jnp.bfloat16)
    spot = lax.broadcasted_iota(jnp.int32, (limit, total), 0).astype(jnp.float32)
    for mb in range(micro):
        w_row = jnp.concatenate(
            [meta[mb * groups + g : mb * groups + g + 1] for g in range(groups)], axis=1
        )
        w_rows = jnp.broadcast_to(w_row, (8, total))
        chosen = jnp.where(w_rows > 0.0, 1.0, 0.0)
        rank = jnp.dot(chosen.astype(jnp.bfloat16), upto, preferred_element_type=jnp.float32)
        rank = jnp.where(w_rows > 0.0, rank - 1.0, -1.0)
        is_at = spot == jnp.broadcast_to(rank[0:1], (limit, total))
        pick[mb] = jnp.where(is_at, 1.0, 0.0).astype(jnp.bfloat16)
        pick_w[mb] = jnp.sum(
            jnp.where(is_at, jnp.broadcast_to(w_row, (limit, total)), 0.0), axis=1, keepdims=True
        )

    @pl.when(sec > 0)
    def _():
        for mb in range(micro):
            relay_copy(mb).wait_recv()
            pack(mb, held[mb])
            peers(lambda p: out_copy(mb, p).start())

    def flat(blocks):
        if cap % 16:
            return blocks.astype(jnp.float32).reshape(total, width).astype(jnp.bfloat16)
        return blocks.reshape(total, width)

    for mb in range(micro):
        peers(lambda p: arrival(arrived.at[mb], d_recv.at[mb], p).wait_recv())
        rows = flat(arrived[mb])
        x = jnp.dot(pick[mb], rows, preferred_element_type=jnp.float32).astype(jnp.bfloat16)
        acc[...] = jnp.zeros_like(acc)

        def chunk_step(c, carry):
            if mb == 0:
                for copy in weight_copies(c):
                    copy.wait()
            gate = jnp.dot(x, wg[c], preferred_element_type=jnp.float32)
            up = jnp.dot(x, wu[c], preferred_element_type=jnp.float32)
            inner = (jax.nn.gelu(gate, approximate=True) * up).astype(jnp.bfloat16)
            acc[...] += jnp.dot(inner, wd[c], preferred_element_type=jnp.float32)
            return carry

        lax.fori_loop(0, FF_CHUNKS, chunk_step, 0)
        scaled = (pick_w[mb] * acc[...]).astype(jnp.bfloat16)
        spread = over_rows(pick[mb], scaled)
        answer[mb] = spread.reshape(n, cap, width).astype(jnp.bfloat16)
        returned[mb, me] = answer[mb, me]
        peers(lambda p: back_copy(mb, p).start())

    for mb in range(micro):
        peers(lambda p: arrival(returned.at[mb], r_recv.at[mb], p).wait_recv())
        sums = []
        for j in range(n_node):
            block = returned[mb, j * n_local].astype(jnp.float32)
            for i in range(1, n_local):
                block = block + returned[mb, j * n_local + i].astype(jnp.float32)
            sums.append(block)
        combined = jnp.concatenate(sums, axis=0).astype(jnp.bfloat16)
        mixed = jnp.dot(hits[mb], combined, preferred_element_type=jnp.float32)
        out_ref[mb] = (held[mb].astype(jnp.float32) + mixed).astype(jnp.bfloat16)

        @pl.when(sec < n_sec - 1)
        def _():
            relay_copy(mb).start()

    def settle(p):
        meta_copy(p).wait_send()
        for mb in range(micro):
            out_copy(mb, p).wait_send()
            back_copy(mb, p).wait_send()

    peers(settle)

    @pl.when(sec < n_sec - 1)
    def _():
        for mb in range(micro):
            relay_copy(mb).wait_send()


def solution(mesh):
    n_sec, n_node, n_local = mesh.shape["section"], mesh.shape["node"], mesh.shape["local"]
    n = n_node * n_local

    def on_device(tokens, expert_ids, slots, gates, gain, w_gate, w_up, w_down):
        micro, toks, width = tokens.shape
        hidden = w_gate.shape[3]
        cap = 2 * toks // n_node
        limit = 4 * toks
        total = n * cap
        chunk = hidden // FF_CHUNKS
        sizes = (n_sec, n_node, n_local, micro, toks, width, cap, limit)
        half, full = jnp.bfloat16, jnp.float32
        vmem = pl.BlockSpec(memory_space=pltpu.VMEM)
        hbm = pl.BlockSpec(memory_space=pl.ANY)
        dma = pltpu.SemaphoreType.DMA
        rows = micro * total // LANES
        out = pl.pallas_call(
            functools.partial(relay_kernel, sizes),
            out_shape=jax.ShapeDtypeStruct((micro, toks, width), half),
            in_specs=[vmem] * 5 + [hbm] * 3,
            out_specs=vmem,
            scratch_shapes=[
                pltpu.VMEM((micro, toks, width), half),
                pltpu.VMEM((micro, n_node, cap, width), half),
                pltpu.VMEM((micro, n, cap, width), half),
                pltpu.VMEM((micro, n, cap, width), half),
                pltpu.VMEM((micro, n, cap, width), half),
                pltpu.VMEM((micro, toks, n_node * cap), half),
                pltpu.VMEM((n, rows, LANES), full),
                pltpu.VMEM((n, rows, LANES), full),
                pltpu.VMEM((micro, limit, total), half),
                pltpu.VMEM((micro, limit, 1), full),
                pltpu.VMEM((limit, width), full),
                pltpu.VMEM((FF_CHUNKS, width, chunk), half),
                pltpu.VMEM((FF_CHUNKS, width, chunk), half),
                pltpu.VMEM((FF_CHUNKS, chunk, width), half),
                dma((3, FF_CHUNKS)),
                dma((n,)), dma((n,)),
                dma((micro, n)), dma((micro, n)),
                dma((micro, n)), dma((micro, n)),
                dma((micro,)), dma((micro,)),
            ],
            compiler_params=pltpu.CompilerParams(collective_id=0, has_side_effects=True),
        )(
            tokens, expert_ids[0], slots[0], gates[0], gain,
            w_gate[0, 0], w_up[0, 0], w_down[0, 0],
        )
        return out[None]

    placed = (
        P(None, ("node", "local"), None),
        P("section", None, ("node", "local"), None),
        P("section", None, ("node", "local"), None),
        P("section", None, ("node", "local"), None),
        P("section", None),
        P("section", ("node", "local"), None, None),
        P("section", ("node", "local"), None, None),
        P("section", ("node", "local"), None, None),
    )
    return jax.shard_map(
        on_device,
        mesh=mesh,
        in_specs=placed,
        out_specs=P("section", None, ("node", "local"), None),
        check_vma=False,
    )
```

time: 222 us -> 93.2 us (0.42)
  the two profiles are of different devices: /device:TPU:0 before, /device:TPU:1 now
where the time goes in v1:
time: 93.2 us; the launch traced here: 92.6 us
  Pallas kernels  86.7 us (93%)
  local copies, waits for them, and re-layouts  5.84 us (6%)
    pallas_call x1, Pallas kernels, on_device(): pl.pallas_call(functools.partial(relay_kernel, sizes), out_shape=jax.Shap...  86.7 us
    unnamed x4, local copies, waits for them, and re-layouts  5.84 us

profile of v1, /device:TPU:1, one launch (start us, length us, event | category | flops | bytes accessed | tf_op | source)
XLA Modules:
  0.0 92.6 jit_solution(12736274834529963220)
XLA Ops:
  0.0 1.4 %copy.9 = s32[1,2,64,2]{3,2,1,0:T(8,128)} copy(s32[1,2,64,2]{2,3,1,0:T(2,128)} %param.9) | data formatting | bytes 2048 | tf_op args[1]
  1.4 1.4 %copy.10 = s32[1,2,64,2]{3,2,1,0:T(8,128)} copy(s32[1,2,64,2]{2,3,1,0:T(2,128)} %param.10) | data formatting | bytes 2048 | tf_op args[2]
  2.8 1.4 %copy.11 = f32[1,2,64,2]{3,2,1,0:T(8,128)} copy(f32[1,2,64,2]{2,3,1,0:T(2,128)} %param.11) | data formatting | bytes 2048 | tf_op args[3]
  4.2 86.7 %shard_map.82 = bf16[2,64,768]{2,1,0:T(8,128)(2,1)} custom-call(bf16[2,64,768]{2,1,0:T(8,128)(2,1)} %tok_ref.1, s32[2,64,2]{2,1,0:T(8,128)} %bitcast.11, s32[2,64,2]{2,1,0:T(8,128)} %bitcast.12, f32[2,64,2]{2,1,0:T(8,128)} %bitcast.13, f32[1,768]{1,0:T(1,128)} %gain_ref.1, bf16[768,3072]{1,0:T(8,128)(2,1)} %bitcast.7, bf16[768,3072]{1,0:T(8,128)(2,1)} %bitcast.8, ...), custom_call_target="tpu_custom_call" | custom-call | tf_op jit(solution)/shard_map/pallas_call | solution.py:250
  90.9 1.6 %copy.13 = bf16[1,2,64,768]{3,2,1,0:T(8,128)(2,1)} copy(bf16[1,2,64,768]{3,2,1,0:T(8,128)(2,1)} %bitcast.10) | data formatting | bytes 393216

commit v2 on v1

--- a/solution.py
+++ b/solution.py
@@ -12,19 +12,14 @@
 FF_CHUNKS = 3
 
 
-def over_rows(a, b, precision=None):
-    return lax.dot_general(
-        a, b, (((0,), (0,)), ((), ())), precision=precision, preferred_element_type=jnp.float32
-    )
-
-
 def relay_kernel(
     sizes,
     tok_ref, ids_ref, slots_ref, gates_ref, gain_ref, wg_hbm, wu_hbm, wd_hbm,
     out_ref,
-    held, packed, arrived, answer, returned, hits, meta_out, meta_in, pick, pick_w, acc,
-    wg, wu, wd,
-    w_sem, meta_send, meta_recv, d_send, d_recv, r_send, r_recv, relay_send, relay_recv,
+    held, packed, arrived, answer, parts, summed, back, hits, hits_t, meta_out, meta_in,
+    pick, pick_t, pick_w, acc, wg, wu, wd,
+    w_sem, meta_send, meta_recv, out_send, out_recv, fan_send, fan_recv,
+    part_send, part_recv, back_send, back_recv, relay_send, relay_recv,
 ):
     n_sec, n_node, n_local, micro, toks, width, cap, limit = sizes
     n = n_node * n_local
@@ -67,22 +62,43 @@
             device_id=device(p), device_id_type=MESH,
         )
 
-    def out_copy(mb, p):
-        return pltpu.make_async_remote_copy(
-            packed.at[mb, lax.div(p, n_local)], arrived.at[mb, me], d_send.at[mb, p],
-            d_recv.at[mb, me], device_id=device(p), device_id_type=MESH,
-        )
-
-    def back_copy(mb, p):
-        return pltpu.make_async_remote_copy(
-            answer.at[mb, p], returned.at[mb, me], r_send.at[mb, p],
-            r_recv.at[mb, me], device_id=device(p), device_id_type=MESH,
-        )
+    def out_copy(mb, j):
+        return pltpu.make_async_remote_copy(
+            packed.at[mb, j], arrived.at[mb, me], out_send.at[mb, j],
+            out_recv.at[mb, me], device_id={"node": j}, device_id_type=MESH,
+        )
+
+    def fan_copy(mb, j, i):
+        block = j * n_local + local
+        return pltpu.make_async_remote_copy(
+            arrived.at[mb, block], arrived.at[mb, block], fan_send.at[mb, j * n_local + i],
+            fan_recv.at[mb, block], device_id={"local": i}, device_id_type=MESH,
+        )
+
+    def part_copy(mb, j, i):
+        return pltpu.make_async_remote_copy(
+            answer.at[mb, j * n_local + i], parts.at[mb, j * n_local + local],
+            part_send.at[mb, j * n_local + i], part_recv.at[mb, j * n_local + local],
+            device_id={"local": i}, device_id_type=MESH,
+        )
+
+    def back_copy(mb, j):
+        return pltpu.make_async_remote_copy(
+            summed.at[mb, j], back.at[mb, node], back_send.at[mb, j],
+            back_recv.at[mb, node], device_id={"node": j}, device_id_type=MESH,
+        )
+
+    def nodes(body):
+        lax.fori_loop(1, n_node, lambda i, c: (body(lax.rem(node + i, n_node)), c)[1], 0)
+
+    def locals_(body):
+        for i in range(1, n_local):
+            body(lax.rem(local + i, n_local))
 
     def arrival(buffer, sem, p):
         return pltpu.make_async_remote_copy(
             buffer.at[p], buffer.at[p], sem.at[p], sem.at[p],
-            device_id=device(p), device_id_type=MESH,
+            device_id={"section": lax.rem(sec + 1, n_sec)}, device_id_type=MESH,
         )
 
     def relay_copy(mb):
@@ -91,9 +107,9 @@
             device_id={"section": lax.rem(sec + 1, n_sec)}, device_id_type=MESH,
         )
 
-    slot_span = lax.broadcasted_iota(jnp.int32, (toks, n_node * cap), 1)
-    exp_span = lax.broadcasted_iota(jnp.int32, (toks, n), 1)
-    lane_span = lax.broadcasted_iota(jnp.int32, (toks, LANES), 1)
+    slot_span = lax.broadcasted_iota(jnp.int32, (n_node * cap, toks), 0)
+    exp_span = lax.broadcasted_iota(jnp.int32, (n, toks), 0)
+    lane_span = lax.broadcasted_iota(jnp.int32, (LANES, toks), 0)
     row_span = lax.broadcasted_iota(jnp.int32, (n, micro * groups, LANES), 1)
     my_group = lax.div(me * cap, LANES)
     my_lane = lax.rem(me * cap, LANES)
@@ -102,20 +118,23 @@
         hit = None
         weights = None
         for k in range(2):
-            e = ids_ref[mb, :, k : k + 1]
-            s = slots_ref[mb, :, k : k + 1]
-            g = gates_ref[mb, :, k : k + 1]
+            e = ids_ref[mb, k : k + 1, :]
+            s = slots_ref[mb, k : k + 1, :]
+            g = gates_ref[mb, k : k + 1, :]
             pos = jnp.where(s >= 0, lax.div(e, jnp.full_like(e, n_local)) * cap + s, -1)
             this = jnp.where(pos == slot_span, 1.0, 0.0)
             hit = this if hit is None else jnp.maximum(hit, this)
             lane = jnp.where(s >= 0, my_lane + s, -1)
-            part = over_rows(
+            part = lax.dot_general(
                 jnp.where(e == exp_span, g, 0.0),
                 jnp.where(lane == lane_span, 1.0, 0.0),
-                lax.Precision.HIGHEST,
+                (((1,), (1,)), ((), ())),
+                precision=lax.Precision.HIGHEST,
+                preferred_element_type=jnp.float32,
             )
             weights = part if weights is None else weights + part
         hits[mb] = hit.astype(jnp.bfloat16)
+        hits_t[mb] = hit.T.astype(jnp.bfloat16)
         meta = meta + jnp.where(row_span == mb * groups + my_group, weights[:, None, :], 0.0)
     meta_out[...] = meta
     meta_in[me] = meta_out[me]
@@ -124,10 +143,23 @@
         floats = h.astype(jnp.float32)
         mean_square = jnp.mean(floats * floats, axis=-1, keepdims=True)
         normed = (floats * lax.rsqrt(mean_square + 1e-05) * gain_ref[...]).astype(jnp.bfloat16)
-        rows = over_rows(hits[mb], normed)
+        rows = jnp.dot(hits[mb], normed, preferred_element_type=jnp.float32)
         for j in range(n_node):
             packed[mb, j] = rows[j * cap : (j + 1) * cap].astype(jnp.bfloat16)
         arrived[mb, me] = packed[mb, node]
+
+    def dispatch(mb):
+        nodes(lambda j: out_copy(mb, j).start())
+        locals_(lambda i: fan_copy(mb, node, i).start())
+
+    def hand_on(mb):
+        def step(i, carry):
+            j = lax.rem(node + n_node - i, n_node)
+            arrival(arrived.at[mb], out_recv.at[mb], j * n_local + local).wait_recv()
+            locals_(lambda k: fan_copy(mb, j, k).start())
+            return carry
+
+        lax.fori_loop(1, n_node, step, 0)
 
     @pl.when(sec == 0)
     def _():
@@ -139,10 +171,12 @@
 
     @pl.when(sec == 0)
     def _():
-        peers(lambda p: out_copy(0, p).start())
+        dispatch(0)
         for mb in range(1, micro):
             pack(mb, held[mb])
-            peers(lambda p: out_copy(mb, p).start())
+            dispatch(mb)
+        for mb in range(micro):
+            hand_on(mb)
 
     peers(lambda p: arrival(meta_in, meta_recv, p).wait_recv())
     meta = jnp.sum(meta_in[...], axis=0)
@@ -160,7 +194,9 @@
         rank = jnp.dot(chosen.astype(jnp.bfloat16), upto, preferred_element_type=jnp.float32)
         rank = jnp.where(w_rows > 0.0, rank - 1.0, -1.0)
         is_at = spot == jnp.broadcast_to(rank[0:1], (limit, total))
-        pick[mb] = jnp.where(is_at, 1.0, 0.0).astype(jnp.bfloat16)
+        place = jnp.where(is_at, 1.0, 0.0)
+        pick[mb] = place.astype(jnp.bfloat16)
+        pick_t[mb] = place.T.astype(jnp.bfloat16)
         pick_w[mb] = jnp.sum(
             jnp.where(is_at, jnp.broadcast_to(w_row, (limit, total)), 0.0), axis=1, keepdims=True
         )
@@ -170,15 +206,23 @@
         for mb in range(micro):
             relay_copy(mb).wait_recv()
             pack(mb, held[mb])
-            peers(lambda p: out_copy(mb, p).start())
+            dispatch(mb)
+            hand_on(mb)
 
     def flat(blocks):
         if cap % 16:
-            return blocks.astype(jnp.float32).reshape(total, width).astype(jnp.bfloat16)
-        return blocks.reshape(total, width)
-
-    for mb in range(micro):
-        peers(lambda p: arrival(arrived.at[mb], d_recv.at[mb], p).wait_recv())
+            return blocks.astype(jnp.float32).reshape(-1, width).astype(jnp.bfloat16)
+        return blocks.reshape(-1, width)
+
+    for mb in range(micro):
+
+        def wait_fan(j, carry):
+            locals_(
+                lambda i: arrival(arrived.at[mb], fan_recv.at[mb], j * n_local + i).wait_recv()
+            )
+            return carry
+
+        lax.fori_loop(0, n_node, wait_fan, 0)
         rows = flat(arrived[mb])
         x = jnp.dot(pick[mb], rows, preferred_element_type=jnp.float32).astype(jnp.bfloat16)
         acc[...] = jnp.zeros_like(acc)
@@ -195,34 +239,47 @@
 
         lax.fori_loop(0, FF_CHUNKS, chunk_step, 0)
         scaled = (pick_w[mb] * acc[...]).astype(jnp.bfloat16)
-        spread = over_rows(pick[mb], scaled)
+        spread = jnp.dot(pick_t[mb], scaled, preferred_element_type=jnp.float32)
         answer[mb] = spread.reshape(n, cap, width).astype(jnp.bfloat16)
-        returned[mb, me] = answer[mb, me]
-        peers(lambda p: back_copy(mb, p).start())
-
-    for mb in range(micro):
-        peers(lambda p: arrival(returned.at[mb], r_recv.at[mb], p).wait_recv())
-        sums = []
-        for j in range(n_node):
-            block = returned[mb, j * n_local].astype(jnp.float32)
+        nodes(lambda j: locals_(lambda i: part_copy(mb, j, i).start()))
+        locals_(lambda i: part_copy(mb, node, i).start())
+
+    for mb in range(micro):
+
+        def add_up(j):
+            rows = answer[mb, j * n_local + local].astype(jnp.float32)
+            locals_(
+                lambda i: arrival(parts.at[mb], part_recv.at[mb], j * n_local + i).wait_recv()
+            )
             for i in range(1, n_local):
-                block = block + returned[mb, j * n_local + i].astype(jnp.float32)
-            sums.append(block)
-        combined = jnp.concatenate(sums, axis=0).astype(jnp.bfloat16)
-        mixed = jnp.dot(hits[mb], combined, preferred_element_type=jnp.float32)
+                block = j * n_local + lax.rem(local + i, n_local)
+                rows = rows + parts[mb, block].astype(jnp.float32)
+            return rows.astype(jnp.bfloat16)
+
+        def send_back(j):
+            summed[mb, j] = add_up(j)
+            back_copy(mb, j).start()
+
+        nodes(send_back)
+        back[mb, node] = add_up(node)
+        nodes(lambda j: arrival(back.at[mb], back_recv.at[mb], j).wait_recv())
+        mixed = jnp.dot(hits_t[mb], flat(back[mb]), preferred_element_type=jnp.float32)
         out_ref[mb] = (held[mb].astype(jnp.float32) + mixed).astype(jnp.bfloat16)
 
         @pl.when(sec < n_sec - 1)
         def _():
             relay_copy(mb).start()
 
-    def settle(p):
-        meta_copy(p).wait_send()
-        for mb in range(micro):
-            out_copy(mb, p).wait_send()
-            back_copy(mb, p).wait_send()
-
-    peers(settle)
+    peers(lambda p: meta_copy(p).wait_send())
+    for mb in range(micro):
+
+        def settle(j):
+            locals_(lambda i: fan_copy(mb, j, i).wait_send())
+            locals_(lambda i: part_copy(mb, j, i).wait_send())
+
+        nodes(lambda j: (out_copy(mb, j).wait_send(), back_copy(mb, j).wait_send()))
+        nodes(settle)
+        settle(node)
 
     @pl.when(sec < n_sec - 1)
     def _():
@@ -258,10 +315,14 @@
                 pltpu.VMEM((micro, n, cap, width), half),
                 pltpu.VMEM((micro, n, cap, width), half),
                 pltpu.VMEM((micro, n, cap, width), half),
+                pltpu.VMEM((micro, n_node, cap, width), half),
+                pltpu.VMEM((micro, n_node, cap, width), half),
+                pltpu.VMEM((micro, n_node * cap, toks), half),
                 pltpu.VMEM((micro, toks, n_node * cap), half),
                 pltpu.VMEM((n, rows, LANES), full),
                 pltpu.VMEM((n, rows, LANES), full),
                 pltpu.VMEM((micro, limit, total), half),
+                pltpu.VMEM((micro, total, limit), half),
                 pltpu.VMEM((micro, limit, 1), full),
                 pltpu.VMEM((limit, width), full),
                 pltpu.VMEM((FF_CHUNKS, width, chunk), half),
@@ -269,13 +330,15 @@
                 pltpu.VMEM((FF_CHUNKS, chunk, width), half),
                 dma((3, FF_CHUNKS)),
                 dma((n,)), dma((n,)),
+                dma((micro, n_node)), dma((micro, n)),
                 dma((micro, n)), dma((micro, n)),
                 dma((micro, n)), dma((micro, n)),
+                dma((micro, n_node)), dma((micro, n_node)),
                 dma((micro,)), dma((micro,)),
             ],
             compiler_params=pltpu.CompilerParams(collective_id=0, has_side_effects=True),
         )(
-            tokens, expert_ids[0], slots[0], gates[0], gain,
+            tokens, *(jnp.swapaxes(a[0], 1, 2) for a in (expert_ids, slots, gates)), gain,
             w_gate[0, 0], w_up[0, 0], w_down[0, 0],
         )
         return out[None]

time: 93.2 us -> 69.4 us (0.74)
  Pallas kernels: 86.7 us -> 67.7 us
  local copies, waits for them, and re-layouts: 5.84 us -> 1.62 us
    pallas_call x1, Pallas kernels: 86.7 us -> 67.7 us  [on_device(): pl.pallas_call(functools.partial(relay_kernel, sizes), out_shape=jax.Shap...]
    unnamed x4 -> x1, local copies, waits for them, and re-layouts: 5.84 us -> 1.62 us
where the time goes in v2:
time: 69.4 us; the launch traced here: 69.3 us
  Pallas kernels  67.7 us (98%)
  local copies, waits for them, and re-layouts  1.62 us (2%)
    pallas_call x1, Pallas kernels, on_device(): pl.pallas_call(functools.partial(relay_kernel, sizes), out_shape=jax.Shap...  67.7 us
    unnamed x1, local copies, waits for them, and re-layouts  1.62 us

profile of v2, /device:TPU:1, one launch (start us, length us, event | category | flops | bytes accessed | tf_op | source)
XLA Modules:
  0.0 69.3 jit_solution(221946645042806553)
XLA Ops:
  0.0 67.7 %shard_map.82 = bf16[2,64,768]{2,1,0:T(8,128)(2,1)} custom-call(bf16[2,64,768]{2,1,0:T(8,128)(2,1)} %tok_ref.1, s32[2,2,64]{2,1,0:T(2,128)} %bitcast.17, s32[2,2,64]{2,1,0:T(2,128)} %bitcast.18, f32[2,2,64]{2,1,0:T(2,128)} %bitcast.19, f32[1,768]{1,0:T(1,128)} %gain_ref.1, bf16[768,3072]{1,0:T(8,128)(2,1)} %bitcast.13, bf16[768,3072]{1,0:T(8,128)(2,1)} %bitcast.14, ...), custom_call_target="tpu_custom_call" | custom-call | tf_op jit(solution)/shard_map/pallas_call | solution.py:307
  67.7 1.6 %copy.10 = bf16[1,2,64,768]{3,2,1,0:T(8,128)(2,1)} copy(bf16[1,2,64,768]{3,2,1,0:T(8,128)(2,1)} %bitcast.16) | data formatting | bytes 393216

commit v3 on v2

--- a/solution.py
+++ b/solution.py
@@ -88,8 +88,17 @@
             back_recv.at[mb, node], device_id={"node": j}, device_id_type=MESH,
         )
 
-    def nodes(body):
-        lax.fori_loop(1, n_node, lambda i, c: (body(lax.rem(node + i, n_node)), c)[1], 0)
+    upper = node >= n_node // 2
+    from_end = jnp.where(upper, node, n_node - 1 - node)
+
+    def nodes(body, near_first=False):
+        def step(i, carry):
+            place = n_node - 2 - i if near_first else i
+            place = jnp.where(place >= from_end, place + 1, place)
+            body(jnp.where(upper, place, n_node - 1 - place))
+            return carry
+
+        lax.fori_loop(0, n_node - 1, step, 0)
 
     def locals_(body):
         for i in range(1, n_local):
@@ -150,16 +159,15 @@
 
     def dispatch(mb):
         nodes(lambda j: out_copy(mb, j).start())
+
+    def hand_on(mb):
         locals_(lambda i: fan_copy(mb, node, i).start())
 
-    def hand_on(mb):
-        def step(i, carry):
-            j = lax.rem(node + n_node - i, n_node)
+        def step(j):
             arrival(arrived.at[mb], out_recv.at[mb], j * n_local + local).wait_recv()
             locals_(lambda k: fan_copy(mb, j, k).start())
-            return carry
-
-        lax.fori_loop(1, n_node, step, 0)
+
+        nodes(step, near_first=True)
 
     @pl.when(sec == 0)
     def _():
@@ -207,7 +215,8 @@
             relay_copy(mb).wait_recv()
             pack(mb, held[mb])
             dispatch(mb)
-            hand_on(mb)
+            if mb == 0:
+                hand_on(mb)
 
     def flat(blocks):
         if cap % 16:
@@ -235,6 +244,13 @@
             up = jnp.dot(x, wu[c], preferred_element_type=jnp.float32)
             inner = (jax.nn.gelu(gate, approximate=True) * up).astype(jnp.bfloat16)
             acc[...] += jnp.dot(inner, wd[c], preferred_element_type=jnp.float32)
+            if mb == 0:
+
+                @pl.when((sec > 0) & (c == 0))
+                def _():
+                    for later in range(1, micro):
+                        hand_on(later)
+
             return carry
 
         lax.fori_loop(0, FF_CHUNKS, chunk_step, 0)
@@ -262,6 +278,8 @@
 
         nodes(send_back)
         back[mb, node] = add_up(node)
+
+    for mb in range(micro):
         nodes(lambda j: arrival(back.at[mb], back_recv.at[mb], j).wait_recv())
         mixed = jnp.dot(hits_t[mb], flat(back[mb]), preferred_element_type=jnp.float32)
         out_ref[mb] = (held[mb].astype(jnp.float32) + mixed).astype(jnp.bfloat16)

time: 69.4 us -> 71.9 us (1.036)
  Pallas kernels: 67.7 us -> 70.1 us
    pallas_call x1, Pallas kernels: 67.7 us -> 70.1 us  [on_device(): pl.pallas_call(functools.partial(relay_kernel, sizes), out_shape=jax.Shap...]
where the time goes in v3:
time: 71.9 us; the launch traced here: 71.8 us
  Pallas kernels  70.1 us (97%)
  local copies, waits for them, and re-layouts  1.62 us (2%)
    pallas_call x1, Pallas kernels, on_device(): pl.pallas_call(functools.partial(relay_kernel, sizes), out_shape=jax.Shap...  70.1 us
    unnamed x1, local copies, waits for them, and re-layouts  1.62 us

profile of v3, /device:TPU:1, one launch (start us, length us, event | category | flops | bytes accessed | tf_op | source)
XLA Modules:
  0.0 71.8 jit_solution(17273919313173748228)
XLA Ops:
  0.0 70.1 %shard_map.82 = bf16[2,64,768]{2,1,0:T(8,128)(2,1)} custom-call(bf16[2,64,768]{2,1,0:T(8,128)(2,1)} %tok_ref.1, s32[2,2,64]{2,1,0:T(2,128)} %bitcast.17, s32[2,2,64]{2,1,0:T(2,128)} %bitcast.18, f32[2,2,64]{2,1,0:T(2,128)} %bitcast.19, f32[1,768]{1,0:T(1,128)} %gain_ref.1, bf16[768,3072]{1,0:T(8,128)(2,1)} %bitcast.13, bf16[768,3072]{1,0:T(8,128)(2,1)} %bitcast.14, ...), custom_call_target="tpu_custom_call" | custom-call | tf_op jit(solution)/shard_map/pallas_call | solution.py:325
  70.1 1.6 %copy.10 = bf16[1,2,64,768]{3,2,1,0:T(8,128)(2,1)} copy(bf16[1,2,64,768]{3,2,1,0:T(8,128)(2,1)} %bitcast.16) | data formatting | bytes 393216
